TPU v7x, 256 devices: a whole 4x4x8 slice. The times are simulated.
256 devices in a mesh: dp: 8 (over z), expert: 32 (over x, y, core).
Axes of the slice: x: 4, y: 4, z: 8, core: 2. Of those that a mesh axis runs over, the one named last changes fastest.
Arguments:
- tokens: bfloat16 [65536, 2048], P(('dp', 'expert')), may hold values from -6 to 6
- expert_ranks: int32 [32, 65536], P(None, ('dp', 'expert')), may hold values from 0 to 65535, as said below
- capacity: int32 [32], replicated, may hold values from 512 to 1024, as said below
- weight_in: bfloat16 [32, 2048, 8192], P('expert', None, 'dp'), may hold values from -0.125 to 0.125
- weight_out: bfloat16 [32, 8192, 2048], P('expert', 'dp'), may hold values from -0.0625 to 0.0625
- gate_weights: float32 [32, 1024], P('expert', 'dp'), may hold values from 0.05 to 1
Outputs:
- combined: bfloat16 [65536, 2048], P(('dp', 'expert'))
Inputs may be any that keep to these rules, and one draw needn't show every extreme that they name: `expert_ranks`: for each expert the ranks are a permutation of 0 to 65535. Of the 256 tokens of one device, at most 8 have rank under 1024 for one expert; for an expert of capacity 1024, some devices have exactly 8. At least one expert has capacity 1024.
All inputs are finite; a program needn't handle non-finite values.
Results may differ from a plain program's by a relative error of at most 0.0053.
Values may be sent and summed in bfloat16 or wider, within the bound.
No kernel may reach another device: no remote copies, remote signals or barrier semaphores. Data moves between devices by JAX's collectives and lax.ppermute only.
A program may use at most 64 MiB of HBM per device.

v0:
```python
import jax
import jax.numpy as jnp
from jax import lax
from jax.sharding import Mesh
from jax.sharding import PartitionSpec as P

MOST = 8
EXPERT = ("expert_0", "expert_1", "expert_2")
DP_EXPERT = ("dp", "expert_0", "expert_1", "expert_2")


def exclusive(values):
    return jnp.cumsum(values) - values


def on_device(tokens, expert_ranks, capacity, weight_in, weight_out, gate_weights):
    dp_count = lax.axis_size("dp")
    expert_count = lax.axis_size(EXPERT)
    token_count, width = tokens.shape
    slots_dp = gate_weights.shape[1]
    rows_all = expert_count * MOST
    own_dp = lax.axis_index("dp")
    own_expert = lax.axis_index(EXPERT)
    chosen = expert_ranks < capacity[:, None]
    chosen_int = chosen.astype(jnp.int32)
    counts = jnp.sum(chosen_int, axis=1)
    before = jnp.cumsum(chosen_int, axis=1) - chosen_int
    places = lax.broadcasted_iota(jnp.int32, (expert_count, MOST, token_count), 1)
    pack_table = jnp.logical_and(chosen[:, None, :], before[:, None, :] == places)
    pack_table = pack_table.astype(jnp.bfloat16).reshape(rows_all, token_count)
    packed = jnp.dot(pack_table, tokens, preferred_element_type=jnp.float32).astype(jnp.bfloat16)
    arrived_rows = lax.all_to_all(
        packed.reshape(expert_count, MOST, width), EXPERT, split_axis=0, concat_axis=0, tiled=True
    ).reshape(rows_all, width)
    device_ids = lax.broadcasted_iota(jnp.int32, (expert_count, expert_count), 0)
    expert_ids = lax.broadcasted_iota(jnp.int32, (expert_count, expert_count), 1)
    table = lax.psum(jnp.where(device_ids == own_expert, counts[None, :], 0), EXPERT)
    plane_ids = lax.broadcasted_iota(jnp.int32, (dp_count, expert_count), 0)
    plane_counts = lax.psum(
        jnp.where(plane_ids == own_dp, jnp.sum(table, axis=0)[None, :], 0), "dp"
    )
    most_rows = jnp.max(plane_counts)
    arrived = jnp.sum(jnp.where(expert_ids == own_expert, table, 0), axis=1)
    earlier = jnp.logical_and(plane_ids < own_dp, expert_ids[:dp_count] == own_expert)
    first_slot = jnp.sum(jnp.where(earlier, plane_counts, 0))
    within = lax.broadcasted_iota(jnp.int32, (expert_count, MOST), 1)
    target = jnp.where(within < arrived[:, None], exclusive(arrived)[:, None] + within, -1).reshape(
        rows_all
    )
    gates_all = lax.all_gather(gate_weights[0], "dp", axis=0, tiled=True)
    gates_all = jnp.concatenate([gates_all, jnp.zeros((rows_all,), gates_all.dtype)])

    def experts(rows, plane_rows):
        slot_ids = lax.broadcasted_iota(jnp.int32, (rows_all, plane_rows), 1)
        place_table = (target[:, None] == slot_ids).astype(jnp.bfloat16)
        plane = lax.dot_general(
            place_table, rows, (((0,), (0,)), ((), ())), preferred_element_type=jnp.float32
        ).astype(jnp.bfloat16)
        slot_rows = lax.all_gather(plane, "dp", axis=0, tiled=True)
        hidden = jnp.maximum(
            jnp.dot(slot_rows, weight_in[0], preferred_element_type=jnp.float32), 0.0
        ).astype(jnp.bfloat16)
        share = jnp.dot(hidden, weight_out[0], preferred_element_type=jnp.float32)
        out = lax.psum_scatter(
            share.astype(jnp.bfloat16), "dp", scatter_dimension=0, tiled=True
        ).astype(jnp.float32)
        gates = lax.dynamic_slice_in_dim(gates_all, first_slot, plane_rows, 0)
        scaled = (gates[:, None] * out).astype(jnp.bfloat16)
        returned = jnp.dot(place_table, scaled, preferred_element_type=jnp.float32)
        return returned.astype(jnp.bfloat16)

    fair = slots_dp + slots_dp // 4
    sent_back = lax.cond(
        most_rows <= fair,
        lambda rows: experts(rows, fair),
        lambda rows: experts(rows, rows_all),
        arrived_rows,
    )
    results = lax.all_to_all(
        sent_back.reshape(expert_count, MOST, width),
        EXPERT,
        split_axis=0,
        concat_axis=0,
        tiled=True,
    ).reshape(rows_all, width)
    combined = lax.dot_general(
        pack_table, results, (((0,), (0,)), ((), ())), preferred_element_type=jnp.float32
    )
    return combined.astype(jnp.bfloat16)


def solution(mesh):
    split = Mesh(
        mesh.devices.reshape(mesh.shape["dp"], 4, 4, 2), ("dp", "expert_0", "expert_1", "expert_2")
    )
    placed = (
        P(DP_EXPERT, None),
        P(None, DP_EXPERT),
        P(),
        P(EXPERT, None, "dp"),
        P(EXPERT, "dp", None),
        P(EXPERT, "dp"),
    )
    return jax.shard_map(
        on_device, mesh=split, in_specs=placed, out_specs=P(DP_EXPERT, None), check_vma=False
    )
```

profile of v0, /device:TPU:1, one launch (start us, length us, event | category | flops | bytes accessed | tf_op | source)
XLA Modules:
  0.0 359.8 jit_solution(15286796204240877624)
XLA Ops:
  6.5 0.9 convert_bitcast_fusion.1
  7.5 0.6 reduce-window.11
  8.1 0.2 slice_reduce_fusion
  8.3 0.1 iota.68
  8.4 0.1 convert_subtract_fusion
  8.5 1.5 fusion.21
  10.0 8.6 %all-to-all-start = ((bf16[32,8,2048]{2,1,0:T(8,128)(2,1)}), bf16[32,8,2048]{2,1,0:T(8,128)(2,1)S(1)}, u32[]{:S(2)}, u32[]{:S(2)}) async-start(bf16[32,8,2048]{2,1,0:T(8,128)(2,1)} %fusion.21), calls=%async_computation.2 | async-start | bytes 2097152 | tf_op jit(solution)/shard_map/all_to_all | solution.py:32
  18.7 127.2 %psum.14 = s32[32,32]{1,0:T(8,128)S(1)} all-reduce(s32[32,32]{1,0:T(8,128)S(1)} %broadcast_select_fusion), channel_id=1, replica_groups=mesh['dp'=8,'expert_0'=4,'expert_1'=4,'expert_2'=2] {'expert_0','expert_..., use_global_device_ids=true, to_apply=%region_3.4 | all-reduce | flops 1024 | bytes 8192 | tf_op jit(solution)/shard_map/psum | solution.py:37
  145.9 0.1 select_reduce_fusion.2
  146.1 13.5 %psum.15 = s32[8,32]{1,0:T(8,128)S(1)} all-reduce(s32[8,32]{1,0:T(8,128)S(1)} %broadcast_select_fusion.1), channel_id=1, replica_groups=mesh['dp'=8,'expert_0'=4,'expert_1'=4,'expert_2'=2] {'dp'}, use_global_device_ids=true, to_apply=%region_5.6 | all-reduce | flops 256 | bytes 2048 | tf_op jit(solution)/shard_map/psum | solution.py:39
  159.6 0.7 reduce_max.9
  161.0 0.1 copy.25
  161.2 10.9 %all-gather = f32[1,1024]{1,0:T(1,128)S(1)} all-gather(f32[1,128]{1,0:T(1,128)S(1)} %copy-done.1), channel_id=2, replica_groups=mesh['dp'=8,'expert_0'=4,'expert_1'=4,'expert_2'=2] {'dp'}, dimensions={1}, use_global_device_ids=true | all-gather | bytes 4608 | tf_op jit(solution)/shard_map/all_gather | solution.py:50
  172.1 155.2 %conditional.2 = (bf16[256,2048]{1,0:T(8,128)(2,1)S(1)}) conditional(s32[]{:T(128)} %convert_element_type.51, (s32[32]{0:T(128)S(1)}, s32[32,8]{1,0:T(8,128)S(1)}, s32[32,1]{1,0:T(8,128)S(1)}, s32[32,8]{1,0:T(8,128)S(1)}, f32[1024]{0:T(1024)S(1)}, /*index=5*/s32[]{:T(128)}, s32[8]{0:T(128)S(1)}, pred[32]{0:T(512)(128)(4,1)S(1)}, ...), branch_computations={%region_9.12_spmd, %region_12.15_spmd} | conditional | flops 17727356928 | bytes 85999704
  172.3 0.1 eq.45
  172.4 1.3 convolution_convert_fusion.3
  173.7 0.2 reduce-scatter.5.cloned.1.call-start
  174.0 70.5 %all-gather.6.cloned.1.call-done = bf16[1280,2048]{1,0:T(8,128)(2,1)} async-done(((bf16[160,2048]{1,0:T(8,128)(2,1)}), bf16[1280,2048]{1,0:T(8,128)(2,1)}) %all-gather.6.cloned.1.call-update) | async-done | bytes 5242896 | tf_op jit(solution)/shard_map/cond/branch_1_fun/all_gather | solution.py:59
  244.4 16.9 %convolution_convert_fusion.2 = bf16[1280,2048]{1,0:T(8,128)(2,1)} fusion(bf16[1,1024,2048]{2,1,0:T(8,128)(2,1)} %get-tuple-element.129, bf16[1280,2048]{1,0:T(8,128)(2,1)} %all-gather.6.cloned.1.call-done, bf16[1,2048,1024]{2,1,0:T(8,128)(2,1)} %get-tuple-element.128), kind=kOutput, calls=%fused_computation.19 | convolution fusion | flops 10742661120 | bytes 18874368 | tf_op jit(solution)/shard_map/cond/branch_1_fun/dot_general | solution.py:63
  261.4 0.7 select_reduce_fusion.1
  264.1 61.4 %reduce-scatter.5.cloned.1.call-done = bf16[160,2048]{1,0:T(8,128)(2,1)} async-done(((bf16[1280,2048]{1,0:T(8,128)(2,1)}), bf16[160,2048]{1,0:T(8,128)(2,1)}) %reduce-scatter.5.cloned.1.call-update) | async-done | bytes 655376 | tf_op jit(solution)/shard_map/cond/branch_1_fun/reduce_scatter | solution.py:64
  325.4 1.6 fusion.15
  327.3 24.3 %all_to_all.10 = bf16[32,8,2048]{2,1,0:T(8,128)(2,1)S(1)} all-to-all(bf16[32,8,2048]{2,1,0:T(8,128)(2,1)S(1)} %bitcast.60), channel_id=1, replica_groups=mesh['dp'=8,'expert_0'=4,'expert_1'=4,'expert_2'=2] {'expert_0','expert_..., dimensions={0} | all-to-all | bytes 2097152 | tf_op jit(solution)/shard_map/all_to_all | solution.py:79
  351.5 1.5 fusion.20
  (25 shorter events, 0.6 us)
Async XLA Ops:
  6.5 2.0 copy-start
  6.5 154.6 %copy-start.1 = (f32[1,128]{1,0:T(1,128)S(1)}, f32[1,128]{1,0:T(1,128)}, u32[]{:S(2)}) copy-start(f32[1,128]{1,0:T(1,128)} %param.13) | copy-start | bytes 1540
  10.0 162.1 %all-to-all-start = ((bf16[32,8,2048]{2,1,0:T(8,128)(2,1)}), bf16[32,8,2048]{2,1,0:T(8,128)(2,1)S(1)}, u32[]{:S(2)}, u32[]{:S(2)}) async-start(bf16[32,8,2048]{2,1,0:T(8,128)(2,1)} %fusion.21), calls=%async_computation.2 | async-start | bytes 2097152 | tf_op jit(solution)/shard_map/all_to_all | solution.py:32
  172.1 72.3 %all-gather.6.cloned.1.call-start = ((), (), s32[]{:S(2)}) async-start(), calls=%async_computation.6 | async-start | bytes 5898240 | tf_op jit(solution)/shard_map/cond/branch_1_fun/all_gather | solution.py:59
  173.7 151.7 %reduce-scatter.5.cloned.1.call-start = ((), (), s32[]{:S(2)}) async-start(), calls=%async_computation.7 | async-start | bytes 5898240 | tf_op jit(solution)/shard_map/cond/branch_1_fun/reduce_scatter | solution.py:64
Sparse Core Ops, SparseCore 0:
  174.7 69.7 all-gather.5
  261.5 63.9 reduce-scatter.4
where the time goes:
time: 360 us
  blocking collectives  176 us (49%)
  waiting for transfers between devices  132 us (37%)
  matrix products  22.7 us (6%)
  between operations  14.1 us (4%)
  starting transfers between devices  8.84 us (2%)
    psum x1, blocking collectives, on_device(): lax.psum(jnp.where(device_ids == own_expert, counts[None, :], 0), EXPERT)  127 us
    all_gather x1, waiting for transfers between devices, experts(): slot_rows = lax.all_gather(plane, 'dp', axis=0, tiled=True)  70.5 us
    reduce_scatter x1, waiting for transfers between devices, experts(): lax.psum_scatter(share.astype(jnp.bfloat16), 'dp', scatter_dimension=0, t...  61.4 us
    all_to_all x1, blocking collectives, on_device(): lax.all_to_all(sent_back.reshape(expert_count, MOST, width), EXPERT, spli...  24.3 us
    dot_general x1, matrix products, experts(): share = jnp.dot(hidden, weight_out[0], preferred_element_type=jnp.float32)  16.9 us
    psum x1, blocking collectives, on_device(): lax.psum(jnp.where(plane_ids == own_dp, jnp.sum(table, axis=0)[None, :],...  13.5 us
    all_gather x1, blocking collectives, on_device(): gates_all = lax.all_gather(gate_weights[0], 'dp', axis=0, tiled=True)  10.9 us
    all_to_all x1, starting transfers between devices, on_device(): lax.all_to_all(packed.reshape(expert_count, MOST, width), EXPERT, split_a...  8.58 us
  transfers between devices with their start and end apart: 3, of which 2 were waited for; matrix products, arithmetic and copies ran while one was open for 1% of the time, Pallas kernels for 0%

commit v1 on v0

--- a/solution.py
+++ b/solution.py
@@ -34,7 +34,8 @@
     ).reshape(rows_all, width)
     device_ids = lax.broadcasted_iota(jnp.int32, (expert_count, expert_count), 0)
     expert_ids = lax.broadcasted_iota(jnp.int32, (expert_count, expert_count), 1)
-    table = lax.psum(jnp.where(device_ids == own_expert, counts[None, :], 0), EXPERT)
+    one_axis = lax.psum(jnp.where(device_ids == own_expert, counts[None, :], 0), "expert_0")
+    table = lax.psum(one_axis, ("expert_1", "expert_2"))
     plane_ids = lax.broadcasted_iota(jnp.int32, (dp_count, expert_count), 0)
     plane_counts = lax.psum(
         jnp.where(plane_ids == own_dp, jnp.sum(table, axis=0)[None, :], 0), "dp"

time: 360 us -> 276 us (0.77)
  blocking collectives: 176 us -> 92.4 us
    psum x1 -> x2, blocking collectives: 127 us -> 44.4 us  [the longest x1 23.6 us: on_device(): table = lax.psum(one_axis, ('expert_1', 'expert_2'))]
where the time goes in v1:
time: 276 us; the launch traced here: 275 us
  waiting for transfers between devices  131 us (47%)
  blocking collectives  92.4 us (33%)
  matrix products  22.7 us (8%)
  between operations  14.1 us (5%)
  starting transfers between devices  8.84 us (3%)
  other arithmetic  3.51 us (1%)
    all_gather x1, waiting for transfers between devices, experts(): slot_rows = lax.all_gather(plane, 'dp', axis=0, tiled=True)  69.3 us
    reduce_scatter x1, waiting for transfers between devices, experts(): lax.psum_scatter(share.astype(jnp.bfloat16), 'dp', scatter_dimension=0, t...  61.3 us
    all_to_all x1, blocking collectives, on_device(): lax.all_to_all(sent_back.reshape(expert_count, MOST, width), EXPERT, spli...  24.3 us
    psum x1, blocking collectives, on_device(): table = lax.psum(one_axis, ('expert_1', 'expert_2'))  23.6 us
    psum x1, blocking collectives, on_device(): lax.psum(jnp.where(device_ids == own_expert, counts[None, :], 0), 'expert...  20.8 us
    dot_general x1, matrix products, experts(): share = jnp.dot(hidden, weight_out[0], preferred_element_type=jnp.float32)  16.9 us
    psum x1, blocking collectives, on_device(): lax.psum(jnp.where(plane_ids == own_dp, jnp.sum(table, axis=0)[None, :],...  13.2 us
    all_gather x1, blocking collectives, on_device(): gates_all = lax.all_gather(gate_weights[0], 'dp', axis=0, tiled=True)  10.6 us
  transfers between devices with their start and end apart: 3, of which 2 were waited for; matrix products, arithmetic and copies ran while one was open for 1% of the time, Pallas kernels for 0%

profile of v1, /device:TPU:1, one launch (start us, length us, event | category | flops | bytes accessed | tf_op | source)
XLA Modules:
  0.0 275.2 jit_solution(12779037291223920106)
XLA Ops:
  6.5 0.9 convert_bitcast_fusion.1
  7.5 0.6 reduce-window.11
  8.1 0.2 slice_reduce_fusion
  8.3 0.1 iota.68
  8.4 0.1 convert_subtract_fusion
  8.5 1.5 fusion.21
  10.0 8.6 %all-to-all-start = ((bf16[32,8,2048]{2,1,0:T(8,128)(2,1)}), bf16[32,8,2048]{2,1,0:T(8,128)(2,1)S(1)}, u32[]{:S(2)}, u32[]{:S(2)}) async-start(bf16[32,8,2048]{2,1,0:T(8,128)(2,1)} %fusion.21), calls=%async_computation.2 | async-start | bytes 2097152 | tf_op jit(solution)/shard_map/all_to_all | solution.py:32
  18.7 20.8 %psum.21 = s32[32,32]{1,0:T(8,128)S(1)} all-reduce(s32[32,32]{1,0:T(8,128)S(1)} %broadcast_select_fusion), channel_id=1, replica_groups=mesh['dp'=8,'expert_0'=4,'expert_1'=4,'expert_2'=2] {'expert_0'}, use_global_device_ids=true, to_apply=%region_3.4 | all-reduce | flops 1024 | bytes 8192 | tf_op jit(solution)/shard_map/psum | solution.py:37
  39.5 23.6 %psum.22 = s32[32,32]{1,0:T(8,128)S(1)} all-reduce(s32[32,32]{1,0:T(8,128)S(1)} %psum.21), channel_id=1, replica_groups=mesh['dp'=8,'expert_0'=4,'expert_1'=4,'expert_2'=2] {'expert_1','expert_2'}, use_global_device_ids=true, to_apply=%region_4.5 | all-reduce | flops 1024 | bytes 8192 | tf_op jit(solution)/shard_map/psum | solution.py:38
  63.1 0.1 select_reduce_fusion.2
  63.2 13.2 %psum.23 = s32[8,32]{1,0:T(8,128)S(1)} all-reduce(s32[8,32]{1,0:T(8,128)S(1)} %broadcast_select_fusion.1), channel_id=1, replica_groups=mesh['dp'=8,'expert_0'=4,'expert_1'=4,'expert_2'=2] {'dp'}, use_global_device_ids=true, to_apply=%region_6.7 | all-reduce | flops 256 | bytes 2048 | tf_op jit(solution)/shard_map/psum | solution.py:40
  76.5 0.7 reduce_max.9
  78.0 10.6 %all-gather = f32[1,1024]{1,0:T(1,128)S(1)} all-gather(f32[1,128]{1,0:T(1,128)S(1)} %copy-done.1), channel_id=2, replica_groups=mesh['dp'=8,'expert_0'=4,'expert_1'=4,'expert_2'=2] {'dp'}, dimensions={1}, use_global_device_ids=true | all-gather | bytes 4608 | tf_op jit(solution)/shard_map/all_gather | solution.py:51
  88.6 154.0 %conditional.2 = (bf16[256,2048]{1,0:T(8,128)(2,1)S(1)}) conditional(s32[]{:T(128)} %convert_element_type.51, (s32[32]{0:T(128)S(1)}, s32[32,8]{1,0:T(8,128)S(1)}, s32[32,1]{1,0:T(8,128)S(1)}, s32[32,8]{1,0:T(8,128)S(1)}, f32[1024]{0:T(1024)S(1)}, /*index=5*/s32[]{:T(128)}, s32[8]{0:T(128)S(1)}, pred[32]{0:T(512)(128)(4,1)S(1)}, ...), branch_computations={%region_10.13_spmd, %region_13.16_spmd} | conditional | flops 17727356928 | bytes 85999704
  88.8 0.1 eq.45
  88.9 1.3 convolution_convert_fusion.3
  90.2 0.2 reduce-scatter.5.cloned.1.call-start
  90.5 69.3 %all-gather.6.cloned.1.call-done = bf16[1280,2048]{1,0:T(8,128)(2,1)} async-done(((bf16[160,2048]{1,0:T(8,128)(2,1)}), bf16[1280,2048]{1,0:T(8,128)(2,1)}) %all-gather.6.cloned.1.call-update) | async-done | bytes 5242896 | tf_op jit(solution)/shard_map/cond/branch_1_fun/all_gather | solution.py:60
  159.8 16.9 %convolution_convert_fusion.2 = bf16[1280,2048]{1,0:T(8,128)(2,1)} fusion(bf16[1,1024,2048]{2,1,0:T(8,128)(2,1)} %get-tuple-element.129, bf16[1280,2048]{1,0:T(8,128)(2,1)} %all-gather.6.cloned.1.call-done, bf16[1,2048,1024]{2,1,0:T(8,128)(2,1)} %get-tuple-element.128), kind=kOutput, calls=%fused_computation.19 | convolution fusion | flops 10742661120 | bytes 18874368 | tf_op jit(solution)/shard_map/cond/branch_1_fun/dot_general | solution.py:64
  176.7 0.7 select_reduce_fusion.1
  179.4 61.3 %reduce-scatter.5.cloned.1.call-done = bf16[160,2048]{1,0:T(8,128)(2,1)} async-done(((bf16[1280,2048]{1,0:T(8,128)(2,1)}), bf16[160,2048]{1,0:T(8,128)(2,1)}) %reduce-scatter.5.cloned.1.call-update) | async-done | bytes 655376 | tf_op jit(solution)/shard_map/cond/branch_1_fun/reduce_scatter | solution.py:65
  240.8 1.6 fusion.15
  242.6 24.3 %all_to_all.10 = bf16[32,8,2048]{2,1,0:T(8,128)(2,1)S(1)} all-to-all(bf16[32,8,2048]{2,1,0:T(8,128)(2,1)S(1)} %bitcast.60), channel_id=1, replica_groups=mesh['dp'=8,'expert_0'=4,'expert_1'=4,'expert_2'=2] {'expert_0','expert_..., dimensions={0} | all-to-all | bytes 2097152 | tf_op jit(solution)/shard_map/all_to_all | solution.py:80
  266.9 1.5 fusion.20
  (26 shorter events, 0.7 us)
Async XLA Ops:
  6.5 2.0 copy-start
  6.5 71.5 %copy-start.1 = (f32[1,128]{1,0:T(1,128)S(1)}, f32[1,128]{1,0:T(1,128)}, u32[]{:S(2)}) copy-start(f32[1,128]{1,0:T(1,128)} %param.13) | copy-start | bytes 1540
  10.0 78.6 %all-to-all-start = ((bf16[32,8,2048]{2,1,0:T(8,128)(2,1)}), bf16[32,8,2048]{2,1,0:T(8,128)(2,1)S(1)}, u32[]{:S(2)}, u32[]{:S(2)}) async-start(bf16[32,8,2048]{2,1,0:T(8,128)(2,1)} %fusion.21), calls=%async_computation.2 | async-start | bytes 2097152 | tf_op jit(solution)/shard_map/all_to_all | solution.py:32
  88.6 71.1 %all-gather.6.cloned.1.call-start = ((), (), s32[]{:S(2)}) async-start(), calls=%async_computation.6 | async-start | bytes 5898240 | tf_op jit(solution)/shard_map/cond/branch_1_fun/all_gather | solution.py:60
  90.2 150.5 %reduce-scatter.5.cloned.1.call-start = ((), (), s32[]{:S(2)}) async-start(), calls=%async_computation.7 | async-start | bytes 5898240 | tf_op jit(solution)/shard_map/cond/branch_1_fun/reduce_scatter | solution.py:65
Sparse Core Ops, SparseCore 0:
  91.2 68.4 all-gather.5
  176.8 63.9 reduce-scatter.4
